TPU v7x, 256 devices: a whole 4x4x8 slice. The times are simulated.
256 devices in a mesh: dp: 32 (over z_hi, y, core), mp: 8 (over z_lo, x).
Axes of the slice: x: 4, y: 4, z: 8 (z_hi: 4, z_lo: 2; z = z_hi * 2 + z_lo), core: 2. Of those that a mesh axis runs over, the one named last changes fastest.
Arguments:
- features: bfloat16 [4096, 4608], P('dp'), may hold values from -6 to 6
- proj_in: bfloat16 [4608, 2560], P('dp', 'mp'), may hold values from -0.09375 to 0.09375
- proj_out: bfloat16 [2560, 2560], P('mp'), may hold values from -0.125 to 0.125
- expert_gate: bfloat16 [64, 2560, 1536], P('dp', None, 'mp'), may hold values from -0.125 to 0.125
- expert_up: bfloat16 [64, 2560, 1536], P('dp', None, 'mp'), may hold values from -0.125 to 0.125
- expert_down: bfloat16 [64, 1536, 2560], P('dp', 'mp'), may hold values from -0.15625 to 0.15625
- routes: int32 [4096, 6], P('dp'), may hold values from 0 to 63, all different within a row; in each aligned block of 128 rows (0 to 127, 128 to 255, ...) at most 15 rows name the same one
- gate_weights: float32 [4096, 6], P('dp'), may hold values from 0.1 to 0.6
- cotangent: bfloat16 [4096, 2560], P('dp'), may hold values from -0.09375 to 0.09375
- first_in: float32 [4608, 2560], P('dp', 'mp'), may hold values from -2 to 2
- second_in: float32 [4608, 2560], P('dp', 'mp'), may hold values from 0.02 to 1
- first_out: float32 [2560, 2560], P('mp', 'dp'), may hold values from -2 to 2
- second_out: float32 [2560, 2560], P('mp', 'dp'), may hold values from 0.02 to 1
Outputs:
- moe_out: bfloat16 [4096, 2560], P('dp')
- new_proj_in: bfloat16 [4608, 2560], P('dp', 'mp')
- new_proj_out: bfloat16 [2560, 2560], P('mp', 'dp')
- new_first_in: float32 [4608, 2560], P('dp', 'mp')
- new_second_in: float32 [4608, 2560], P('dp', 'mp')
- new_first_out: float32 [2560, 2560], P('mp', 'dp')
- new_second_out: float32 [2560, 2560], P('mp', 'dp')
Inputs may be any that keep to these rules, and one draw needn't show every extreme that they name: `routes`: each row names 6 different experts. Within the rows of one device (aligned blocks of 128 rows) no expert is named more than 15 times, and in every draw some expert is named exactly 15 times in some block.
All inputs are finite; a program needn't handle non-finite values.
Results may differ from a plain program's by a relative error of at most 0.01.
Values may be sent and summed in bfloat16 or wider, within the bound.
No kernel may reach another device: no remote copies, remote signals or barrier semaphores. Data moves between devices by JAX's collectives and lax.ppermute only.
A program may use at most 128 MiB of HBM per device.

v0:
```python
import jax
import jax.numpy as jnp
from jax import lax
from jax.sharding import PartitionSpec as P

EXPERTS = 64
TOP = 6
CAP = 15
BETA_ONE = 0.9
BETA_TWO = 0.999
EPSILON = 1e-08
LEARN_RATE = 0.001
WEIGHT_DECAY = 0.1
FIRST_FIX = 1.0 - 0.9**50 * 0.9**50
SECOND_FIX = 1.0 - 0.999**50 * 0.999**50


def in_blocks(value, dim, peers):
    before, after = (value.shape[:dim], value.shape[dim + 1 :])
    return jnp.moveaxis(value.reshape(*before, peers, -1, *after), dim, 0)


def sent_and_summed(value, axis, dim):
    pieces = in_blocks(value, dim, lax.axis_size(axis))
    arrived = lax.all_to_all(pieces, axis, split_axis=0, concat_axis=0, tiled=True)
    return arrived.sum(axis=0)


def sent_together(arrays, axis, split_dim, concat_dim, along):
    widths = [a.shape[along] for a in arrays]
    both = jnp.concatenate(arrays, axis=along)
    out = lax.all_to_all(both, axis, split_axis=split_dim, concat_axis=concat_dim, tiled=True)
    return tuple(jnp.split(out, [sum(widths[:k]) for k in range(1, len(widths))], axis=along))


def sent_together_2(arrays, axis, dim, along):
    both = jnp.concatenate(arrays, axis=along)
    out, at, done = (lax.psum_scatter(both, axis, scatter_dimension=dim, tiled=True), 0, [])
    for a in arrays:
        done.append(lax.slice_in_dim(out, at, at + a.shape[along], axis=along))
        at += a.shape[along]
    return tuple(done)


def turned_gather(arrays, axis, dims):
    turned = [jnp.moveaxis(a, dim, 0) for a, dim in zip(arrays, dims)]
    widths = [t[0].size for t in turned]
    both = jnp.concatenate([t.reshape(-1, w) for t, w in zip(turned, widths)], axis=1)
    out = lax.all_gather(both, axis, axis=0, tiled=True)
    pieces = jnp.split(out, [sum(widths[:k]) for k in range(1, len(widths))], axis=1)
    return tuple(
        (
            jnp.moveaxis(b.reshape(-1, *t.shape[1:]), 0, dim)
            for b, t, dim in zip(pieces, turned, dims)
        )
    )


def gelu_parts(preact):

    def smooth(values):
        return jax.nn.gelu(values, approximate=True)

    result, pullback = jax.vjp(smooth, preact)
    return (result, pullback(jnp.ones_like(preact))[0])


def slot_table(chosen_block):
    chosen = chosen_block.reshape(-1)
    onehot = (chosen[:, None] == jnp.arange(EXPERTS, dtype=jnp.int32)[None, :]).astype(jnp.int32)
    earlier = jnp.cumsum(onehot, axis=0) - onehot
    return (chosen, jnp.sum(earlier * onehot, axis=1))


def adamw_update(weight, gradient, first, second):
    first_new = BETA_ONE * first + (1.0 - BETA_ONE) * gradient
    second_new = BETA_TWO * second + (1.0 - BETA_TWO) * gradient * gradient
    update = first_new / FIRST_FIX / (jnp.sqrt(second_new / SECOND_FIX) + EPSILON)
    current = weight.astype(jnp.float32)
    return (
        (current - LEARN_RATE * (update + WEIGHT_DECAY * current)).astype(jnp.bfloat16),
        first_new,
        second_new,
    )


def expert_pass(inputs, grads_in, w_gate, w_up, w_down):
    gate_projection = jnp.einsum("erd,edf->erf", inputs, w_gate, preferred_element_type=jnp.float32)
    up_projection = jnp.einsum("erd,edf->erf", inputs, w_up, preferred_element_type=jnp.float32)
    sigmoid_gate = jax.nn.sigmoid(gate_projection)
    silu_gate = gate_projection * sigmoid_gate
    inner_activation = (silu_gate * up_projection).astype(jnp.bfloat16)
    out_part = jnp.einsum(
        "erf,efd->erd", inner_activation, w_down, preferred_element_type=jnp.float32
    ).astype(jnp.bfloat16)
    down_weight_gradient = jnp.einsum(
        "erd,efd->erf", grads_in, w_down, preferred_element_type=jnp.float32
    )
    gate_weight_gradient = (
        down_weight_gradient
        * up_projection
        * sigmoid_gate
        * (1.0 + gate_projection * (1.0 - sigmoid_gate))
    ).astype(jnp.bfloat16)
    up_weight_gradient = (down_weight_gradient * silu_gate).astype(jnp.bfloat16)
    input_part = (
        jnp.einsum("erf,edf->erd", gate_weight_gradient, w_gate, preferred_element_type=jnp.float32)
        + jnp.einsum("erf,edf->erd", up_weight_gradient, w_up, preferred_element_type=jnp.float32)
    ).astype(jnp.bfloat16)
    return (out_part, input_part)


def slot_sources(position, flat_weights, total_slots):
    pair_count = position.shape[0]
    owner = (
        jnp.zeros((total_slots,), jnp.int32)
        .at[position]
        .set(jnp.arange(pair_count, dtype=jnp.int32) + 1)
    )
    live = owner > 0
    pair_id = jnp.maximum(owner - 1, 0)
    source_row = pair_id // TOP
    slot_weight = jnp.where(live, flat_weights[pair_id], 0.0)
    return (live, source_row, slot_weight)


def fill_inputs(rows, live, source_row):
    return jnp.where(live[:, None], rows[source_row], jnp.zeros((), rows.dtype))


def fill_grads(grads, slot_weight, source_row):
    return (slot_weight[:, None] * grads[source_row].astype(jnp.float32)).astype(jnp.bfloat16)


def collect_rows(buffer, pair_slots, pair_weights):
    flat = buffer.reshape(-1, buffer.shape[-1])
    total = jnp.zeros((pair_slots.shape[0], flat.shape[1]), jnp.float32)
    for choice_index in range(TOP):
        picked = flat[pair_slots[:, choice_index]]
        if pair_weights is None:
            total = total + picked
        else:
            total = total + pair_weights[:, choice_index : choice_index + 1] * picked
    return total


def local(
    features,
    proj_in,
    proj_out,
    expert_gate,
    expert_up,
    expert_down,
    routes,
    gate_weights,
    cotangent,
    first_in,
    second_in,
    first_out,
    second_out,
):
    row_count = features.shape[0]
    model_width = cotangent.shape[1]
    data_parts = lax.axis_size("dp")
    model_parts = lax.axis_size("mp")
    data_place = lax.axis_index("dp")
    model_place = lax.axis_index("mp")
    column_width = model_width // model_parts
    column_start = model_place * column_width
    own_experts = expert_gate.shape[0]
    total_slots = own_experts * data_parts * CAP
    expert_rows = data_parts * CAP
    preact = jnp.dot(
        features,
        lax.all_gather(proj_in, "dp", axis=0, tiled=True),
        preferred_element_type=jnp.float32,
    )
    activated, gelu_slope = gelu_parts(preact)
    hidden = activated.astype(jnp.bfloat16)
    partial_value = jnp.dot(hidden, proj_out, preferred_element_type=jnp.float32)
    chosen, slot_index = slot_table(routes)
    position = chosen * CAP + slot_index
    pair_slots = position.reshape(row_count, TOP)
    live, source_row, slot_weight = slot_sources(position, gate_weights.reshape(-1), total_slots)
    cotangent_cols = lax.dynamic_slice_in_dim(cotangent, column_start, column_width, 1)
    mapped_cols = sent_and_summed(partial_value, "mp", 1).astype(jnp.bfloat16)
    send_rows = fill_inputs(mapped_cols, live, source_row)
    send_grads = fill_grads(cotangent_cols, slot_weight, source_row)
    send_shape = (data_parts, own_experts, CAP, column_width)
    narrow_rows, narrow_grads = sent_together(
        (send_rows.reshape(send_shape), send_grads.reshape(send_shape)), "dp", 0, 2, 1
    )
    recv_rows, recv_grads = (
        lax.all_gather(narrow_rows, "mp", axis=3, tiled=True),
        lax.all_gather(narrow_grads, "mp", axis=3, tiled=True),
    )
    out_part, input_part = expert_pass(
        recv_rows.reshape(own_experts, expert_rows, model_width),
        recv_grads.reshape(own_experts, expert_rows, model_width),
        expert_gate,
        expert_up,
        expert_down,
    )
    back_shape = (1, own_experts, expert_rows, model_width)
    summed_out, summed_in = tuple(
        (
            part.astype(jnp.float32)
            for part in sent_together_2(
                (
                    out_part.astype(jnp.float32).reshape(back_shape).astype(jnp.bfloat16),
                    input_part.astype(jnp.float32).reshape(back_shape).astype(jnp.bfloat16),
                ),
                "mp",
                3,
                0,
            )
        )
    )
    back_out, back_in = sent_together((summed_out, summed_in), "dp", 2, 0, 1)
    moe_cols = (
        mapped_cols.astype(jnp.float32) + collect_rows(back_out, pair_slots, gate_weights)
    ).astype(jnp.bfloat16)
    grad_cols = (
        cotangent_cols.astype(jnp.float32) + collect_rows(back_in, pair_slots, None)
    ).astype(jnp.bfloat16)
    moe_out, grad_mapped = turned_gather((moe_cols, grad_cols), "mp", (1, 1))
    grad_hidden = lax.dot_general(
        grad_mapped, proj_out, (((1,), (1,)), ((), ())), preferred_element_type=jnp.float32
    )
    grad_pre = (grad_hidden * gelu_slope).astype(jnp.bfloat16)
    vis_part = features.shape[1] // data_parts
    width_part = model_width // data_parts
    share_rows = vis_part + width_part
    feature_blocks = features.reshape(row_count, data_parts, vis_part)
    mapped_blocks = grad_mapped.reshape(row_count, data_parts, width_part)
    term_in = jnp.einsum(
        "tnv,th->nvh", feature_blocks, grad_pre, preferred_element_type=jnp.float32
    )
    term_out = jnp.einsum("tnd,th->ndh", mapped_blocks, hidden, preferred_element_type=jnp.float32)
    shares = lax.psum_scatter(
        jnp.concatenate([term_in, term_out], axis=1)
        .reshape(share_rows * lax.axis_size("dp"), hidden.shape[1])
        .astype(jnp.bfloat16),
        "dp",
        scatter_dimension=0,
        tiled=True,
    ).astype(jnp.float32)
    grad_in = shares[:vis_part]
    grad_out = shares[vis_part:].T
    own_out = lax.dynamic_slice_in_dim(proj_out, data_place * width_part, width_part, 1)
    new_in, first_in_new, second_in_new = adamw_update(proj_in, grad_in, first_in, second_in)
    new_out, first_out_new, second_out_new = adamw_update(own_out, grad_out, first_out, second_out)
    return (moe_out, new_in, new_out, first_in_new, second_in_new, first_out_new, second_out_new)


def solution(mesh):
    return jax.shard_map(
        local,
        mesh=mesh,
        in_specs=(
            P("dp", None),
            P("dp", "mp"),
            P("mp", None),
            P("dp", None, "mp"),
            P("dp", None, "mp"),
            P("dp", "mp", None),
            P("dp", None),
            P("dp", None),
            P("dp", None),
            P("dp", "mp"),
            P("dp", "mp"),
            P("mp", "dp"),
            P("mp", "dp"),
        ),
        out_specs=(
            P("dp", None),
            P("dp", "mp"),
            P("mp", "dp"),
            P("dp", "mp"),
            P("dp", "mp"),
            P("mp", "dp"),
            P("mp", "dp"),
        ),
        check_vma=False,
    )
```

profile of v0, /device:TPU:2, one launch (start us, length us, event | category | flops | bytes accessed | tf_op | source)
XLA Modules:
  0.0 869.0 jit_solution(17863692709619640517)
XLA Ops:
  7.9 64.8 %all-gather.5.cloned.1.call-done = bf16[4608,320]{1,0:T(8,128)(2,1)} async-done(((bf16[144,320]{1,0:T(8,128)(2,1)}), bf16[4608,320]{1,0:T(8,128)(2,1)}) %all-gather.5.cloned.1.call-update) | async-done | bytes 2949136 | tf_op jit(solution)/shard_map/all_gather | solution.py:175
  72.7 3.9 fusion.81
  76.6 2.0 fusion.73
  78.6 4.9 all-to-all-start
  84.0 1.8 reduce-window.6
  87.2 3.4 scatter_custom_fusion
  91.6 5.0 gather_fusion.2
  100.3 4.8 gather_fusion.1
  106.5 1.4 broadcast_in_dim.22
  107.9 1.8 multiply_convert_fusion
  111.3 5.0 gather_fusion
  116.3 1.5 gather.48
  119.8 38.4 %all_to_all.41 = bf16[32,4,15,320]{3,1,2,0:T(4,128)(2,1)S(1)} all-to-all(bf16[32,4,15,320]{3,1,2,0:T(4,128)(2,1)S(1)} %copy.84), channel_id=1, replica_groups=mesh['dp'=32,'mp'=8] {'dp'}, dimensions={0} | all-to-all | bytes 2457600 | tf_op jit(solution)/shard_map/all_to_all | solution.py:32
  159.3 2.2 copy.85
  161.6 2.3 copy.87
  164.2 61.7 %all-gather.7.cloned.1.call-done = bf16[1,2,480,2560]{2,1,0,3:T(2,128)(2,1)} async-done(((bf16[1,2,480,320]{2,1,0,3:T(2,128)(2,1)}), bf16[1,2,480,2560]{2,1,0,3:T(2,128)(2,1)}) %all-gather.7.cloned.1.call-update) | async-done | bytes 4915216 | tf_op jit(solution)/shard_map/all_gather | solution.py:194
  225.9 13.7 %copy.86 = bf16[1,2,480,2560]{3,2,1,0:T(8,128)(2,1)} copy(bf16[1,2,480,2560]{2,1,0,3:T(2,128)(2,1)} %all-gather.7.cloned.1.call-done) | data formatting | bytes 9830400 | tf_op jit(solution)/shard_map/all_gather | solution.py:194
  239.7 4.8 fusion.4
  244.8 2.4 fusion.2
  247.2 44.2 %all-gather.9.cloned.1.call-done = bf16[1,2,480,2560]{2,1,0,3:T(2,128)(2,1)} async-done(((bf16[1,2,480,320]{2,1,0,3:T(2,128)(2,1)}), bf16[1,2,480,2560]{2,1,0,3:T(2,128)(2,1)}) %all-gather.9.cloned.1.call-update) | async-done | bytes 4915216 | tf_op jit(solution)/shard_map/all_gather | solution.py:195
  291.4 13.8 %copy.88 = bf16[1,2,480,2560]{3,2,1,0:T(8,128)(2,1)} copy(bf16[1,2,480,2560]{2,1,0,3:T(2,128)(2,1)} %all-gather.9.cloned.1.call-done) | data formatting | bytes 9830400 | tf_op jit(solution)/shard_map/all_gather | solution.py:195
  305.2 4.0 fusion
  309.2 3.7 fusion.6
  313.0 1.5 fusion.11
  314.5 3.7 fusion.7
  318.2 8.4 pad_maximum_fusion
  326.7 26.2 %copy.89 = bf16[2,2,480,2560]{2,1,0,3:T(2,128)(2,1)} copy(bf16[2,2,480,2560]{3,2,1,0:T(8,128)(2,1)} %pad_maximum_fusion) | data formatting | bytes 19660800 | tf_op jit(solution)/shard_map/concatenate | solution.py:37
  354.8 226.2 %all-reduce.3.cloned.1.call-done = bf16[2,2,480,2560]{2,1,0,3:T(2,128)(2,1)} async-done(((bf16[2,2,480,2560]{2,1,0,3:T(2,128)(2,1)}), bf16[2,2,480,2560]{2,1,0,3:T(2,128)(2,1)}) %all-reduce.3.cloned.1.call-update) | async-done | bytes 9830416
  581.0 2.2 constant_dynamic-slice_fusion
  583.4 1.7 maximum_convert_fusion
  585.1 4.4 copy.92
  589.5 10.1 %all-to-all-start.2 = ((f32[1,4,480,320]{3,1,0,2:T(4,128)}), f32[1,4,480,320]{3,1,0,2:T(4,128)}, u32[]{:S(2)}, u32[]{:S(2)}) async-start(f32[1,4,480,320]{3,1,0,2:T(4,128)} %copy.92), calls=%async_computation.2 | async-start | bytes 5898240 | tf_op jit(solution)/shard_map/all_to_all | solution.py:32
  600.7 68.1 %all-to-all-done.2 = f32[1,4,480,320]{3,1,0,2:T(4,128)} async-done(((f32[1,4,480,320]{3,1,0,2:T(4,128)}), f32[1,4,480,320]{3,1,0,2:T(4,128)}, u32[]{:S(2)}, u32[]{:S(2)}) %all-to-all-start.2) | async-done | bytes 2457632 | tf_op jit(solution)/shard_map/all_to_all | solution.py:32
  668.9 4.0 fusion.78
  674.2 1.5 reshape.116
  680.0 1.5 reshape.115
  685.9 1.4 gather_fusion.11
  688.7 1.4 gather_fusion.10
  690.2 1.4 gather_fusion.4
  691.6 1.4 gather_fusion.9
  693.9 1.5 fusion.44
  696.5 37.9 %all-gather.11.cloned.1.call-done = bf16[2560,256]{1,0:T(8,128)(2,1)} async-done(((bf16[320,256]{1,0:T(8,128)(2,1)}), bf16[2560,256]{1,0:T(8,128)(2,1)}) %all-gather.11.cloned.1.call-update) | async-done | bytes 1310736 | tf_op jit(solution)/shard_map/all_gather | solution.py:49
  734.4 2.2 fusion.80
  737.8 6.9 fusion.9
  744.7 3.4 convert_bitcast_fusion
  748.1 3.0 pad_maximum_fusion.1
  753.6 105.0 %reduce-scatter.2.cloned.1.call-done = bf16[224,320]{1,0:T(8,128)(2,1)} async-done(((bf16[7168,320]{1,0:T(8,128)(2,1)}), bf16[224,320]{1,0:T(8,128)(2,1)}) %reduce-scatter.2.cloned.1.call-update) | async-done | bytes 143376 | tf_op jit(solution)/shard_map/reduce_scatter | solution.py:240
  860.5 1.7 fusion.41
  (123 shorter events, 35.1 us)
Async XLA Ops:
  7.2 298.0 %copy-start = (bf16[2,192,2560]{2,1,0:T(8,128)(2,1)S(1)}, bf16[2,192,2560]{2,1,0:T(8,128)(2,1)}, u32[]{:S(2)}) copy-start(bf16[2,192,2560]{2,1,0:T(8,128)(2,1)} %param.18) | copy-start | bytes 5898244
  7.2 65.5 %all-gather.5.cloned.1.call-start = ((), (), s32[]{:S(2)}) async-start(), calls=%async_computation.4 | async-start | bytes 3649536 | tf_op jit(solution)/shard_map/all_gather | solution.py:175
  72.7 3.9 copy-start.7
  76.6 2.0 copy-start.12
  78.6 4.9 copy-start.24
  78.6 31.2 %all-to-all-start = ((f32[8,128,320]{1,2,0:T(8,128)}), f32[8,128,320]{1,2,0:T(8,128)}, u32[]{:S(2)}, u32[]{:S(2)}) async-start(f32[8,128,320]{1,2,0:T(8,128)} %bitcast.1), calls=%async_computation | async-start | bytes 2621440 | tf_op jit(solution)/shard_map/all_to_all | solution.py:25
  83.5 142.4 %all-gather.7.cloned.1.call-start = ((), (), s32[]{:S(2)}) async-start(), calls=%async_computation.5 | async-start | bytes 5898240 | tf_op jit(solution)/shard_map/all_gather | solution.py:194
  96.6 1.4 copy-start.22
  111.3 6.5 copy-start.21
  117.8 1.1 copy-start.10
  161.6 129.9 %all-gather.9.cloned.1.call-start = ((), (), s32[]{:S(2)}) async-start(), calls=%async_computation.6 | async-start | bytes 5898240 | tf_op jit(solution)/shard_map/all_gather | solution.py:195
  163.9 417.1 %all-reduce.3.cloned.1.call-start = ((), (), s32[]{:S(2)}) async-start(), calls=%async_computation.9 | async-start | bytes 20971520
  239.6 4.8 copy-start.2
  239.7 5.2 copy-start.4
  305.2 4.0 copy-start.6
  309.2 3.7 copy-start.3
  313.0 1.6 copy-start.5
  352.9 0.7 copy-start.27
  589.5 10.4 %copy-start.9 = (s32[128,6]{1,0:T(8,128)S(1)}, s32[128,6]{1,0:T(8,128)}, u32[]{:S(2)}) copy-start(s32[128,6]{1,0:T(8,128)} %get-tuple-element.43) | copy-start | bytes 9220
  589.5 10.7 %copy-start.23 = (f32[128,6]{0,1:T(8,128)S(1)}, f32[128,6]{0,1:T(8,128)}, u32[]{:S(2)}) copy-start(f32[128,6]{0,1:T(8,128)} %param.20) | copy-start | bytes 9220
  589.5 79.4 %all-to-all-start.2 = ((f32[1,4,480,320]{3,1,0,2:T(4,128)}), f32[1,4,480,320]{3,1,0,2:T(4,128)}, u32[]{:S(2)}, u32[]{:S(2)}) async-start(f32[1,4,480,320]{3,1,0,2:T(4,128)} %copy.92), calls=%async_computation.2 | async-start | bytes 5898240 | tf_op jit(solution)/shard_map/all_to_all | solution.py:32
  599.6 134.8 %all-gather.11.cloned.1.call-start = ((), (), s32[]{:S(2)}) async-start(), calls=%async_computation.7 | async-start | bytes 1474560 | tf_op jit(solution)/shard_map/all_gather | solution.py:49
  693.1 2.3 copy-start.14
  693.1 2.3 copy-start.15
  693.1 2.3 copy-start.16
  693.1 2.3 copy-start.25
  693.1 2.3 copy-start.26
  695.6 41.0 %copy-start.13 = (f32[128,320]{0,1:T(8,128)S(1)}, f32[128,320]{0,1:T(8,128)}, u32[]{:S(2)}) copy-start(f32[128,320]{0,1:T(8,128)} %copy-done.12) | copy-start | bytes 491524
  696.4 162.2 %reduce-scatter.2.cloned.1.call-start = ((), (), s32[]{:S(2)}) async-start(), calls=%async_computation.8 | async-start | bytes 5677056 | tf_op jit(solution)/shard_map/reduce_scatter | solution.py:240
  736.6 1.3 copy-start.8
  751.1 1.3 copy-start.11
  751.2 108.4 %copy-start.17 = (bf16[144,320]{1,0:T(8,128)(2,1)S(1)}, bf16[144,320]{1,0:T(8,128)(2,1)}, u32[]{:S(2)}) copy-start(bf16[144,320]{1,0:T(8,128)(2,1)} %param.14) | copy-start | bytes 276484
  751.2 108.4 %copy-start.18 = (f32[144,320]{1,0:T(8,128)S(1)}, f32[144,320]{1,0:T(8,128)}, u32[]{:S(2)}) copy-start(f32[144,320]{1,0:T(8,128)} %param.22) | copy-start | bytes 552964
  751.2 108.4 %copy-start.19 = (f32[144,320]{1,0:T(8,128)S(1)}, f32[144,320]{1,0:T(8,128)}, u32[]{:S(2)}) copy-start(f32[144,320]{1,0:T(8,128)} %param.23) | copy-start | bytes 552964
  751.2 109.3 %copy-start.20 = (f32[320,80]{0,1:T(8,128)S(1)}, f32[320,80]{0,1:T(8,128)}, u32[]{:S(2)}) copy-start(f32[320,80]{0,1:T(8,128)} %param.24) | copy-start | bytes 307204
  752.3 109.8 %copy-start.1 = (bf16[2,192,2560]{2,1,0:T(8,128)(2,1)S(1)}, bf16[2,192,2560]{2,1,0:T(8,128)(2,1)}, u32[]{:S(2)}) copy-start(bf16[2,192,2560]{2,1,0:T(8,128)(2,1)} %param.18) | copy-start | bytes 5898244
Sparse Core Ops, SparseCore 0:
  10.6 62.0 all-gather.4
  161.7 64.1 all-gather.6
  227.7 63.6 all-gather.8
  353.1 227.9 all-reduce.2
  696.6 37.7 all-gather.10
  751.3 107.2 reduce-scatter.1
where the time goes:
time: 871 us; the launch traced here: 869 us
  waiting for transfers between devices  609 us (70%)
  local copies, waits for them, and re-layouts  128 us (15%)
  blocking collectives  38.4 us (4%)
  matrix products  33.6 us (4%)
  other arithmetic  29.7 us (3%)
  starting transfers between devices  15.6 us (2%)
  between operations  15.3 us (2%)
    unnamed x7, waiting for transfers between devices  227 us
    reduce_scatter x1, waiting for transfers between devices, local(): lax.psum_scatter(jnp.concatenate([term_in, term_out], axis=1).reshape(sha...  105 us
    all_to_all x1, waiting for transfers between devices, sent_together(): lax.all_to_all(both, axis, split_axis=split_dim, concat_axis=concat_dim,...  68.1 us
    all_gather x1, waiting for transfers between devices, local(): lax.all_gather(proj_in, 'dp', axis=0, tiled=True)  64.8 us
    all_gather x1, waiting for transfers between devices, local(): lax.all_gather(narrow_rows, 'mp', axis=3, tiled=True)  61.7 us
    all_gather x1, waiting for transfers between devices, local(): lax.all_gather(narrow_grads, 'mp', axis=3, tiled=True)  44.2 us
    all_to_all x1, blocking collectives, sent_together(): lax.all_to_all(both, axis, split_axis=split_dim, concat_axis=concat_dim,...  38.4 us
    all_gather x1, waiting for transfers between devices, turned_gather(): out = lax.all_gather(both, axis, axis=0, tiled=True)  37.9 us
  transfers between devices with their start and end apart: 8, of which 7 were waited for; matrix products, arithmetic and copies ran while one was open for 6% of the time, Pallas kernels for 0%

commit v1 on v0

--- a/solution.py
+++ b/solution.py
@@ -172,7 +172,9 @@
     expert_rows = data_parts * CAP
     preact = jnp.dot(
         features,
-        lax.all_gather(proj_in, "dp", axis=0, tiled=True),
+        jnp.concatenate(
+            lax.all_to_all(jnp.stack([proj_in] * lax.axis_size("dp")), "dp", 0, 0), axis=0
+        ),
         preferred_element_type=jnp.float32,
     )
     activated, gelu_slope = gelu_parts(preact)

time: 871 us -> 902 us (1.036)
  blocking collectives: 38.4 us -> 130 us
  waiting for transfers between devices: 609 us -> 543 us
    all_to_all x0 -> x1, blocking collectives: none -> 93 us  [local(): lax.all_to_all(jnp.stack([proj_in] * lax.axis_size('dp')), 'dp', 0, 0)]
    all_gather x1 -> x0, waiting for transfers between devices: 64.8 us -> none  [local(): lax.all_gather(proj_in, 'dp', axis=0, tiled=True)]
    unnamed x7 -> x6, waiting for transfers between devices: 227 us -> 226 us
  transfers between devices with their start and end apart: 8 -> 7, of which waited for: 7 -> 6; matrix products, arithmetic and copies ran while one was open for 6% -> 6% of each run, Pallas kernels for 0% -> 0%
where the time goes in v1:
time: 902 us; the launch traced here: 899 us
  waiting for transfers between devices  543 us (60%)
  local copies, waits for them, and re-layouts  130 us (14%)
  blocking collectives  130 us (14%)
  other arithmetic  32.3 us (4%)
  matrix products  31.2 us (3%)
  starting transfers between devices  16.9 us (2%)
  between operations  15 us (2%)
    unnamed x6, waiting for transfers between devices  226 us
    reduce_scatter x1, waiting for transfers between devices, local(): lax.psum_scatter(jnp.concatenate([term_in, term_out], axis=1).reshape(sha...  105 us
    all_to_all x1, blocking collectives, local(): lax.all_to_all(jnp.stack([proj_in] * lax.axis_size('dp')), 'dp', 0, 0)  93 us
    all_to_all x1, waiting for transfers between devices, sent_together(): lax.all_to_all(both, axis, split_axis=split_dim, concat_axis=concat_dim,...  68.1 us
    all_gather x1, waiting for transfers between devices, local(): lax.all_gather(narrow_rows, 'mp', axis=3, tiled=True)  61.8 us
    all_gather x1, waiting for transfers between devices, local(): lax.all_gather(narrow_grads, 'mp', axis=3, tiled=True)  44.2 us
    all_gather x1, waiting for transfers between devices, turned_gather(): out = lax.all_gather(both, axis, axis=0, tiled=True)  37.9 us
    all_to_all x1, blocking collectives, sent_together(): lax.all_to_all(both, axis, split_axis=split_dim, concat_axis=concat_dim,...  37.4 us
  transfers between devices with their start and end apart: 7, of which 6 were waited for; matrix products, arithmetic and copies ran while one was open for 6% of the time, Pallas kernels for 0%

profile of v1, /device:TPU:2, one launch (start us, length us, event | category | flops | bytes accessed | tf_op | source)
XLA Modules:
  0.0 898.9 jit_solution(14335757240744219276)
XLA Ops:
  8.5 93.0 %all_to_all.46 = bf16[32,144,320]{2,1,0:T(8,128)(2,1)S(1)} all-to-all(bf16[32,144,320]{2,1,0:T(8,128)(2,1)S(1)} %stack.2), channel_id=1, replica_groups=mesh['dp'=32,'mp'=8] {'dp'}, dimensions={0} | all-to-all | bytes 5898240 | tf_op jit(solution)/shard_map/all_to_all | solution.py:176
  101.6 1.4 fusion.81
  103.0 2.0 fusion.73
  105.0 6.4 all-to-all-start.1
  112.5 4.4 reduce-window.6
  121.0 3.4 scatter_custom_fusion
  125.4 5.0 gather_fusion.2
  130.4 2.5 reshape.125
  133.1 4.3 gather_fusion.1
  137.8 2.5 multiply_convert_fusion
  140.4 5.0 gather_fusion
  145.4 1.5 gather.48
  149.0 37.4 %all_to_all.47 = bf16[32,4,15,320]{3,1,2,0:T(4,128)(2,1)S(1)} all-to-all(bf16[32,4,15,320]{3,1,2,0:T(4,128)(2,1)S(1)} %copy.84), channel_id=1, replica_groups=mesh['dp'=32,'mp'=8] {'dp'}, dimensions={0} | all-to-all | bytes 2457600 | tf_op jit(solution)/shard_map/all_to_all | solution.py:32
  186.3 1.9 fusion.79
  188.2 3.6 copy.85
  191.9 2.3 copy.87
  194.5 61.8 %all-gather.4.cloned.1.call-done = bf16[1,2,480,2560]{2,1,0,3:T(2,128)(2,1)} async-done(((bf16[1,2,480,320]{2,1,0,3:T(2,128)(2,1)}), bf16[1,2,480,2560]{2,1,0,3:T(2,128)(2,1)}) %all-gather.4.cloned.1.call-update) | async-done | bytes 4915216 | tf_op jit(solution)/shard_map/all_gather | solution.py:196
  256.2 13.7 %copy.86 = bf16[1,2,480,2560]{3,2,1,0:T(8,128)(2,1)} copy(bf16[1,2,480,2560]{2,1,0,3:T(2,128)(2,1)} %all-gather.4.cloned.1.call-done) | data formatting | bytes 9830400 | tf_op jit(solution)/shard_map/all_gather | solution.py:196
  269.9 4.8 fusion.4
  275.1 2.4 fusion.2
  277.5 44.2 %all-gather.6.cloned.1.call-done = bf16[1,2,480,2560]{2,1,0,3:T(2,128)(2,1)} async-done(((bf16[1,2,480,320]{2,1,0,3:T(2,128)(2,1)}), bf16[1,2,480,2560]{2,1,0,3:T(2,128)(2,1)}) %all-gather.6.cloned.1.call-update) | async-done | bytes 4915216 | tf_op jit(solution)/shard_map/all_gather | solution.py:197
  321.8 13.8 %copy.88 = bf16[1,2,480,2560]{3,2,1,0:T(8,128)(2,1)} copy(bf16[1,2,480,2560]{2,1,0,3:T(2,128)(2,1)} %all-gather.6.cloned.1.call-done) | data formatting | bytes 9830400 | tf_op jit(solution)/shard_map/all_gather | solution.py:197
  335.5 4.0 fusion
  339.5 3.7 fusion.6
  343.3 1.5 fusion.11
  344.9 3.7 fusion.7
  348.6 8.4 pad_maximum_fusion
  357.0 26.2 %copy.89 = bf16[2,2,480,2560]{2,1,0,3:T(2,128)(2,1)} copy(bf16[2,2,480,2560]{3,2,1,0:T(8,128)(2,1)} %pad_maximum_fusion) | data formatting | bytes 19660800 | tf_op jit(solution)/shard_map/concatenate | solution.py:37
  385.1 226.2 %all-reduce.3.cloned.1.call-done = bf16[2,2,480,2560]{2,1,0,3:T(2,128)(2,1)} async-done(((bf16[2,2,480,2560]{2,1,0,3:T(2,128)(2,1)}), bf16[2,2,480,2560]{2,1,0,3:T(2,128)(2,1)}) %all-reduce.3.cloned.1.call-update) | async-done | bytes 9830416
  611.3 2.2 constant_dynamic-slice_fusion
  613.7 1.8 maximum_convert_fusion
  615.4 4.4 copy.92
  619.8 10.0 %all-to-all-start.3 = ((f32[1,4,480,320]{3,1,0,2:T(4,128)}), f32[1,4,480,320]{3,1,0,2:T(4,128)}, u32[]{:S(2)}, u32[]{:S(2)}) async-start(f32[1,4,480,320]{3,1,0,2:T(4,128)} %copy.92), calls=%async_computation.3 | async-start | bytes 5898240 | tf_op jit(solution)/shard_map/all_to_all | solution.py:32
  630.9 68.1 %all-to-all-done.3 = f32[1,4,480,320]{3,1,0,2:T(4,128)} async-done(((f32[1,4,480,320]{3,1,0,2:T(4,128)}), f32[1,4,480,320]{3,1,0,2:T(4,128)}, u32[]{:S(2)}, u32[]{:S(2)}) %all-to-all-start.3) | async-done | bytes 2457632 | tf_op jit(solution)/shard_map/all_to_all | solution.py:32
  699.0 4.0 fusion.78
  704.4 1.5 reshape.122
  710.1 1.5 reshape.121
  717.5 1.4 gather_fusion.5
  718.9 1.4 gather_fusion.10
  721.8 1.4 gather_fusion.9
  724.0 1.5 fusion.44
  726.7 37.9 %all-gather.8.cloned.1.call-done = bf16[2560,256]{1,0:T(8,128)(2,1)} async-done(((bf16[320,256]{1,0:T(8,128)(2,1)}), bf16[2560,256]{1,0:T(8,128)(2,1)}) %all-gather.8.cloned.1.call-update) | async-done | bytes 1310736 | tf_op jit(solution)/shard_map/all_gather | solution.py:49
  764.5 2.2 fusion.80
  768.0 6.9 fusion.9
  774.9 3.4 convert_bitcast_fusion
  778.3 3.0 pad_maximum_fusion.1
  783.8 105.0 %reduce-scatter.2.cloned.1.call-done = bf16[224,320]{1,0:T(8,128)(2,1)} async-done(((bf16[7168,320]{1,0:T(8,128)(2,1)}), bf16[224,320]{1,0:T(8,128)(2,1)}) %reduce-scatter.2.cloned.1.call-update) | async-done | bytes 143376 | tf_op jit(solution)/shard_map/reduce_scatter | solution.py:242
  890.7 1.7 fusion.41
  (122 shorter events, 33.7 us)
Async XLA Ops:
  7.2 328.4 %copy-start = (bf16[2,192,2560]{2,1,0:T(8,128)(2,1)S(1)}, bf16[2,192,2560]{2,1,0:T(8,128)(2,1)}, u32[]{:S(2)}) copy-start(bf16[2,192,2560]{2,1,0:T(8,128)(2,1)} %param.18) | copy-start | bytes 5898244
  8.5 93.0 %copy-start.8 = (bf16[128,4608]{1,0:T(8,128)(2,1)S(1)}, bf16[128,4608]{1,0:T(8,128)(2,1)}, u32[]{:S(2)}) copy-start(bf16[128,4608]{1,0:T(8,128)(2,1)} %param.13) | copy-start | bytes 3538948
  101.6 1.5 copy-start.7
  103.0 2.0 copy-start.12
  105.0 6.4 copy-start.22
  105.0 35.2 %all-to-all-start.1 = ((f32[8,128,320]{1,2,0:T(8,128)}), f32[8,128,320]{1,2,0:T(8,128)S(1)}, u32[]{:S(2)}, u32[]{:S(2)}) async-start(f32[8,128,320]{1,2,0:T(8,128)} %bitcast.102), calls=%async_computation.1 | async-start | bytes 2621440 | tf_op jit(solution)/shard_map/all_to_all | solution.py:25
  111.4 144.9 %all-gather.4.cloned.1.call-start = ((), (), s32[]{:S(2)}) async-start(), calls=%async_computation.5 | async-start | bytes 5898240 | tf_op jit(solution)/shard_map/all_gather | solution.py:196
  130.4 2.5 copy-start.21
  146.9 1.1 copy-start.10
  191.9 129.9 %all-gather.6.cloned.1.call-start = ((), (), s32[]{:S(2)}) async-start(), calls=%async_computation.6 | async-start | bytes 5898240 | tf_op jit(solution)/shard_map/all_gather | solution.py:197
  194.3 417.1 %all-reduce.3.cloned.1.call-start = ((), (), s32[]{:S(2)}) async-start(), calls=%async_computation.9 | async-start | bytes 20971520
  269.9 4.8 copy-start.2
  269.9 5.2 copy-start.4
  335.5 4.0 copy-start.6
  339.5 3.8 copy-start.3
  343.3 1.6 copy-start.5
  383.2 0.7 copy-start.27
  619.8 79.2 %all-to-all-start.3 = ((f32[1,4,480,320]{3,1,0,2:T(4,128)}), f32[1,4,480,320]{3,1,0,2:T(4,128)}, u32[]{:S(2)}, u32[]{:S(2)}) async-start(f32[1,4,480,320]{3,1,0,2:T(4,128)} %copy.92), calls=%async_computation.3 | async-start | bytes 5898240 | tf_op jit(solution)/shard_map/all_to_all | solution.py:32
  629.8 134.8 %all-gather.8.cloned.1.call-start = ((), (), s32[]{:S(2)}) async-start(), calls=%async_computation.7 | async-start | bytes 1474560 | tf_op jit(solution)/shard_map/all_gather | solution.py:49
  723.2 2.3 copy-start.14
  723.2 2.3 copy-start.15
  723.2 2.3 copy-start.16
  723.2 2.3 copy-start.23
  723.2 2.3 copy-start.24
  723.2 2.3 copy-start.25
  723.2 2.3 copy-start.26
  725.8 41.0 %copy-start.13 = (f32[128,320]{0,1:T(8,128)S(1)}, f32[128,320]{0,1:T(8,128)}, u32[]{:S(2)}) copy-start(f32[128,320]{0,1:T(8,128)} %copy-done.12) | copy-start | bytes 491524
  726.6 162.2 %reduce-scatter.2.cloned.1.call-start = ((), (), s32[]{:S(2)}) async-start(), calls=%async_computation.8 | async-start | bytes 5677056 | tf_op jit(solution)/shard_map/reduce_scatter | solution.py:242
  766.7 1.3 copy-start.9
  781.3 1.3 copy-start.11
  781.4 108.4 %copy-start.17 = (bf16[144,320]{1,0:T(8,128)(2,1)S(1)}, bf16[144,320]{1,0:T(8,128)(2,1)}, u32[]{:S(2)}) copy-start(bf16[144,320]{1,0:T(8,128)(2,1)} %param.14) | copy-start | bytes 276484
  781.4 108.4 %copy-start.18 = (f32[144,320]{1,0:T(8,128)S(1)}, f32[144,320]{1,0:T(8,128)}, u32[]{:S(2)}) copy-start(f32[144,320]{1,0:T(8,128)} %param.22) | copy-start | bytes 552964
  781.4 108.4 %copy-start.19 = (f32[144,320]{1,0:T(8,128)S(1)}, f32[144,320]{1,0:T(8,128)}, u32[]{:S(2)}) copy-start(f32[144,320]{1,0:T(8,128)} %param.23) | copy-start | bytes 552964
  781.4 109.3 %copy-start.20 = (f32[320,80]{0,1:T(8,128)S(1)}, f32[320,80]{0,1:T(8,128)}, u32[]{:S(2)}) copy-start(f32[320,80]{0,1:T(8,128)} %param.24) | copy-start | bytes 307204
  782.5 109.8 %copy-start.1 = (bf16[2,192,2560]{2,1,0:T(8,128)(2,1)S(1)}, bf16[2,192,2560]{2,1,0:T(8,128)(2,1)}, u32[]{:S(2)}) copy-start(bf16[2,192,2560]{2,1,0:T(8,128)(2,1)} %param.18) | copy-start | bytes 5898244
Sparse Core Ops, SparseCore 0:
  192.0 64.1 all-gather.3
  258.0 63.6 all-gather.5
  383.4 227.8 all-reduce.2
  726.8 37.7 all-gather.7
  781.5 107.2 reduce-scatter.1
